TPU v7x, 32 devices: a whole 2x2x4 slice. The times are simulated.
32 devices in a mesh: cell: 8 (over y, x, core), gene: 4 (over z).
Axes of the slice: x: 2, y: 2, z: 4, core: 2. Of those that a mesh axis runs over, the one named last changes fastest.
Arguments:
- counts: int32 [3072, 8192], P('gene', 'cell'), may hold values from 0 to 11
- batch_id: int32 [8192], P('cell'), may hold values from 0 to 63
- live_cells: int32 [8], P('cell'), may hold values from 256 to 1024, as said below
- knot_bin: int32 [8192], P('cell'), may hold values from 0 to 14
- depth_frac: float32 [8192], P('cell'), may hold values from 0 to 1
- cell_covariates: float32 [16, 8192], P(None, 'cell'), may hold values from -3 to 3
- coefficients: float32 [3072, 32], P('gene'), may hold values from -1.2 to 1.2
- batch_effect: float32 [3072, 64], P('gene'), may hold values from -1.8 to 1.8
- factors: bfloat16 [8192, 64], P('cell'), may hold values from -4 to 4
- loadings: bfloat16 [3072, 64], P('gene'), may hold values from -0.19921875 to 0.19921875
Outputs:
- beta_step: float32 [3072, 32], P('gene')
- factor_step: float32 [8192, 64], P('cell')
- loading_score: float32 [3072, 64], P('gene')
Inputs may be any that keep to these rules, and one draw needn't show every extreme that they name: `live_cells`: each index of the cell axis has its live cells in its first slots, at least 256 of them; some index is full in every draw.
All inputs are finite; a program needn't handle non-finite values.
Results may differ from a plain program's by a relative error of at most 0.0003.
Values sent between devices are 32-bit elements; how exact they have to be, the bound alone decides.
A program may use at most 64 MiB of HBM per device.

v0:
```python
import jax
import jax.numpy as jnp
from jax import lax
from jax.sharding import PartitionSpec as P

GENES = 3072
SPL = 16
BATCHES = 64


ridge_weight = 1.0


def design_rows(knot_bin, depth_frac, cell_covariates):
    levels = jnp.arange(SPL, dtype=jnp.int32)[:, None]
    fraction = depth_frac[None, :]
    hat_basis = jnp.where(levels == knot_bin[None, :], 1.0 - fraction, 0.0)
    hat_basis = hat_basis + jnp.where(levels == knot_bin[None, :] + 1, fraction, 0.0)
    return jnp.concatenate([hat_basis, cell_covariates], axis=0)


def newton_solve(gram_flat, score):
    columns = score.shape[-1]
    identity = jnp.eye(columns, dtype=gram_flat.dtype)
    system = gram_flat.reshape(-1, columns, columns) + ridge_weight * identity
    factor_lower = jnp.linalg.cholesky(system)
    middle = jax.scipy.linalg.solve_triangular(factor_lower, score[..., None], lower=True)
    return jax.scipy.linalg.solve_triangular(factor_lower, middle, lower=True, trans=1)[..., 0]


def local(
    counts,
    batch_id,
    live_cells,
    knot_bin,
    depth_frac,
    cell_covariates,
    coefficients,
    batch_effect,
    factors,
    loadings,
):
    highest = lax.Precision.HIGHEST
    contract = (((1,), (1,)), ((), ()))
    observed = counts.astype(jnp.float32)
    totals = lax.psum(jnp.sum(observed, axis=0), "gene")
    offset = jnp.log((1.0 + totals) / GENES)
    slot_count = observed.shape[1]
    live_mask = (jnp.arange(slot_count, dtype=jnp.int32) < live_cells[0]).astype(jnp.float32)
    design = design_rows(knot_bin, depth_frac, cell_covariates)
    columns = design.shape[0]
    onehot = (jnp.arange(BATCHES, dtype=jnp.int32)[:, None] == batch_id[None, :]).astype(
        jnp.float32
    )
    stacked = jnp.concatenate([design, onehot], axis=0)
    linear = jnp.dot(
        jnp.concatenate([coefficients, batch_effect], axis=1), stacked, precision=highest
    )
    latent = lax.dot_general(loadings, factors, contract, preferred_element_type=jnp.float32)
    linear_pred = offset[None, :] + linear + latent
    expected = jnp.exp(linear_pred)
    weight = expected * live_mask
    residual = (observed - expected) * live_mask
    pairs = (design[:, None, :] * design[None, :, :]).reshape(columns * columns, slot_count)
    gram_part = lax.dot_general(weight, pairs, contract, precision=highest)
    score_part = lax.dot_general(residual, design, contract, precision=highest)
    gram_share, score_share = (
        lax.psum_scatter(gram_part, "cell", scatter_dimension=0, tiled=True),
        lax.psum_scatter(score_part, "cell", scatter_dimension=0, tiled=True),
    )
    step_share = newton_solve(gram_share, score_share)
    beta_step = lax.all_gather(step_share, "cell", axis=0, tiled=True)
    expected_next = jnp.exp(linear_pred + jnp.dot(beta_step, design, precision=highest))
    weight_next = expected_next * live_mask
    residual_next = (observed - expected_next) * live_mask
    factors_wide = factors.astype(jnp.float32)
    loads_wide = loadings.astype(jnp.float32)
    grad_load = jnp.dot(residual_next, factors_wide, precision=highest)
    curv_load = jnp.dot(weight_next, factors_wide * factors_wide, precision=highest)
    back = (((0,), (0,)), ((), ()))
    grad_fact = lax.dot_general(residual_next, loads_wide, back, precision=highest)
    curv_fact = lax.dot_general(weight_next, loads_wide * loads_wide, back, precision=highest)
    grad_load, curv_load = lax.psum((grad_load, curv_load), "cell")
    grad_fact, curv_fact = lax.psum((grad_fact, curv_fact), "gene")
    factor_step = grad_fact / (curv_fact + 1.0)
    loading_score = grad_load / jnp.sqrt(curv_load + 1.0)
    return (beta_step, factor_step, loading_score)


def solution(mesh):
    placed = (
        P("gene", "cell"),
        P("cell"),
        P("cell"),
        P("cell"),
        P("cell"),
        P(None, "cell"),
        P("gene", None),
        P("gene", None),
        P("cell", None),
        P("gene", None),
    )
    return jax.shard_map(
        local,
        mesh=mesh,
        in_specs=placed,
        out_specs=(P("gene", None), P("cell", None), P("gene", None)),
        check_vma=False,
    )
```

profile of v0, /device:TPU:0, one launch (start us, length us, event | category | flops | bytes accessed | tf_op | source)
XLA Modules:
  0.0 549.3 jit_solution(7010824040929546472)
XLA Ops:
  8.7 1.4 fusion.31
  10.1 2.2 convert_reduce_fusion
  12.3 13.5 %psum.35 = f32[1024]{0:T(1024)S(1)} all-reduce(f32[1024]{0:T(1024)S(1)} %convert_reduce_fusion), channel_id=1, replica_groups=mesh['cell'=8,'gene'=4] {'gene'}, use_global_device_ids=true, to_apply=%region_1.0 | all-reduce | flops 1024 | bytes 8192 | tf_op jit(solution)/shard_map/psum | solution.py:46
  27.2 4.0 add_add_fusion
  31.2 3.6 fusion
  35.6 12.0 %fusion.3 = f32[768,1024]{1,0:T(8,128)} fusion(f32[1024,1024]{1,0:T(8,128)S(1)} %bitcast.29, f32[768,1024]{1,0:T(8,128)S(1)} %add_add_fusion, f32[1024]{0:T(1024)S(1)} %fusion.35), kind=kOutput, calls=%fused_computation.5 | convolution fusion | flops 9664462848 | bytes 10489856 | tf_op jit(solution)/shard_map/dot_general | solution.py:65
  47.9 19.2 %reduce-scatter.7.cloned.1.call-done = f32[96,32]{1,0:T(8,128)} async-done(((f32[768,32]{1,0:T(8,128)}), f32[96,32]{1,0:T(8,128)}) %reduce-scatter.7.cloned.1.call-update) | async-done | bytes 12304
  68.0 48.6 %reduce-scatter.5.cloned.1.call-done = f32[96,1024]{1,0:T(8,128)} async-done(((f32[768,1024]{1,0:T(8,128)}), f32[96,1024]{1,0:T(8,128)}) %reduce-scatter.5.cloned.1.call-update) | async-done | bytes 393232 | tf_op jit(solution)/shard_map/reduce_scatter | solution.py:68
  116.6 1.2 copy.43
  118.8 1.4 copy.44
  120.2 2.4 copy.45
  122.6 1.5 fusion.12
  124.1 281.8 %custom-call.11 = f32[96,32,32]{2,1,0:T(8,128)S(1)} custom-call(f32[96,32,32]{2,1,0:T(8,128)} %fusion.12), custom_call_target="Cholesky" | custom-call | tf_op jit(solution)/shard_map/jit(cholesky)/cholesky | solution.py:26
  407.3 12.5 %custom-call.12 = f32[96,1,32,32]{0,2,3,1:T(8,128)S(1)} custom-call(f32[96,1,32,32]{0,3,2,1:T(8,128)S(1)} %select_bitcast_fusion), custom_call_target="InvertDiagBlocksLowerTriangular" | custom-call | tf_op jit(solution)/shard_map/jit(_solve_triangular)/vmap()/triangular_solve | solution.py:28
  420.0 9.2 %all-gather = f32[8,96,32]{1,2,0:T(8,128)S(1)} all-gather(f32[1,96,32]{1,2,0:T(8,128)S(1)} %bitcast.31), channel_id=1, replica_groups=mesh['cell'=8,'gene'=4] {'cell'}, dimensions={0}, use_global_device_ids=true | all-gather | bytes 110592 | tf_op jit(solution)/shard_map/all_gather | solution.py:72
  430.0 4.9 add_exponential_fusion
  434.9 2.7 fusion.17
  437.6 3.8 fusion.6
  441.4 4.1 fusion.18
  445.6 2.9 fusion.8
  448.6 51.6 %all-reduce.5.cloned.1.call-done = (f32[768,64]{0,1:T(8,128)}, f32[768,64]{0,1:T(8,128)}) async-done(((f32[768,64]{0,1:T(8,128)}, f32[768,64]{0,1:T(8,128)}), (f32[768,64]{0,1:T(8,128)}, f32[768,64]{0,1:T(8,128)})) %all-reduce.5.cloned.1.call-update) | async-done | bytes 393232 | tf_op jit(solution)/shard_map/psum | solution.py:83
  500.2 1.7 rsqrt_multiply_fusion
  501.9 39.1 %all-reduce.7.cloned.1.call-done = (f32[1024,64]{0,1:T(8,128)}, f32[1024,64]{0,1:T(8,128)}) async-done(((f32[1024,64]{0,1:T(8,128)}, f32[1024,64]{0,1:T(8,128)}), (f32[1024,64]{0,1:T(8,128)}, f32[1024,64]{0,1:T(8,128)})) %all-reduce.7.cloned.1.call-update) | async-done | bytes 524304 | tf_op jit(solution)/shard_map/psum | solution.py:84
  541.0 1.8 add_divide_fusion
  (49 shorter events, 7.5 us)
Async XLA Ops:
  7.2 19.3 %copy-start.9 = (s32[1024]{0:T(1024)S(1)}, s32[1024]{0:T(1024)}, u32[]{:S(2)}) copy-start(s32[1024]{0:T(1024)} %param.13) | copy-start | bytes 12292
  7.2 19.3 %copy-start.8 = (f32[1024]{0:T(1024)S(1)}, f32[1024]{0:T(1024)}, u32[]{:S(2)}) copy-start(f32[1024]{0:T(1024)} %param.14) | copy-start | bytes 12292
  7.2 19.4 %copy-start.4 = (bf16[1024,64]{0,1:T(8,128)(2,1)S(1)}, bf16[1024,64]{0,1:T(8,128)(2,1)}, u32[]{:S(2)}) copy-start(bf16[1024,64]{0,1:T(8,128)(2,1)} %param.18) | copy-start | bytes 393220
  7.2 19.4 %copy-start.7 = (bf16[768,64]{0,1:T(8,128)(2,1)S(1)}, bf16[768,64]{0,1:T(8,128)(2,1)}, u32[]{:S(2)}) copy-start(bf16[768,64]{0,1:T(8,128)(2,1)} %param.19) | copy-start | bytes 294916
  7.2 59.9 %reduce-scatter.7.cloned.1.call-start = ((), (), s32[]{:S(2)}) async-start(), calls=%async_computation.3 | async-start | bytes 442368
  10.1 17.1 %copy-start.5 = (f32[16,1024]{1,0:T(8,128)S(1)}, f32[16,1024]{1,0:T(8,128)}, u32[]{:S(2)}) copy-start(f32[16,1024]{1,0:T(8,128)} %param.15) | copy-start | bytes 196612
  25.8 1.4 copy-start.6
  27.2 4.0 copy-start
  31.2 4.4 copy-start.2
  34.9 81.7 %reduce-scatter.5.cloned.1.call-start = ((), (), s32[]{:S(2)}) async-start(), calls=%async_computation.2 | async-start | bytes 3538944 | tf_op jit(solution)/shard_map/reduce_scatter | solution.py:68
  47.6 452.6 %all-reduce.5.cloned.1.call-start = ((), (), s32[]{:S(2)}) async-start(), calls=%async_computation.4 | async-start | bytes 786432 | tf_op jit(solution)/shard_map/psum | solution.py:83
  118.0 0.8 copy-start.3
  430.0 4.9 copy-start.1
  445.6 95.4 %all-reduce.7.cloned.1.call-start = ((), (), s32[]{:S(2)}) async-start(), calls=%async_computation.5 | async-start | bytes 1048576 | tf_op jit(solution)/shard_map/psum | solution.py:84
Sparse Core Ops, SparseCore 0:
  35.0 32.0 reduce-scatter.6
  70.5 46.0 reduce-scatter.4
  445.7 54.4 all-reduce.4
  503.0 37.9 all-reduce.6
where the time goes:
time: 550 us; the launch traced here: 549 us
  other arithmetic  306 us (56%)
  waiting for transfers between devices  159 us (29%)
  matrix products  38.7 us (7%)
  blocking collectives  22.7 us (4%)
  between operations  14.7 us (3%)
  local copies, waits for them, and re-layouts  8.44 us (2%)
    another operation x4, other arithmetic, newton_solve(): factor_lower = jnp.linalg.cholesky(system)  282 us
    psum x1, waiting for transfers between devices, local(): grad_load, curv_load = lax.psum((grad_load, curv_load), 'cell')  51.6 us
    reduce_scatter x1, waiting for transfers between devices, local(): lax.psum_scatter(gram_part, 'cell', scatter_dimension=0, tiled=True)  48.6 us
    psum x1, waiting for transfers between devices, local(): grad_fact, curv_fact = lax.psum((grad_fact, curv_fact), 'gene')  39.1 us
    unnamed x5, waiting for transfers between devices  19.3 us
    psum x1, blocking collectives, local(): totals = lax.psum(jnp.sum(observed, axis=0), 'gene')  13.5 us
    another operation x4, other arithmetic, newton_solve(): jax.scipy.linalg.solve_triangular(factor_lower, middle, lower=True, trans=1)  12.8 us
    dot_general x1, matrix products, local(): gram_part = lax.dot_general(weight, pairs, contract, precision=highest)  12 us
  transfers between devices with their start and end apart: 4, of which 4 were waited for; matrix products, arithmetic and copies ran while one was open for 3% of the time, Pallas kernels for 0%

commit v1 on v0

--- a/solution.py
+++ b/solution.py
@@ -1,6 +1,10 @@
+import functools
+
 import jax
 import jax.numpy as jnp
 from jax import lax
+from jax.experimental import pallas as pl
+from jax.experimental.pallas import tpu as pltpu
 from jax.sharding import PartitionSpec as P
 
 GENES = 3072
@@ -28,7 +32,7 @@
     return jax.scipy.linalg.solve_triangular(factor_lower, middle, lower=True, trans=1)[..., 0]
 
 
-def local(
+def local_plain(
     counts,
     batch_id,
     live_cells,
@@ -87,6 +91,542 @@
     return (beta_step, factor_step, loading_score)
 
 
+MESH = pl.DeviceIdType.MESH
+F32, BF16 = jnp.float32, jnp.bfloat16
+VM = pl.BlockSpec(memory_space=pltpu.VMEM)
+ROWS_BY_ROWS = (((1,), (1,)), ((), ()))
+ACROSS = (((1,), (0,)), ((), ()))
+DOWN = (((0,), (0,)), ((), ()))
+LIMIT = 60 * 1024 * 1024
+
+
+def split(x):
+    high = x.astype(BF16)
+    return high, (x - high.astype(F32)).astype(BF16)
+
+
+def mul(a, b, dims):
+    return lax.dot_general(a, b, dims, preferred_element_type=F32)
+
+
+def remote(src, dst, send, recv, where):
+    return pltpu.make_async_remote_copy(
+        src_ref=src, dst_ref=dst, send_sem=send, recv_sem=recv, device_id=where, device_id_type=MESH
+    )
+
+
+def meet(groups):
+    barrier = pltpu.get_barrier_semaphore()
+    count = 0
+    for axis, n in groups:
+        me = lax.axis_index(axis)
+        for d in range(1, n):
+            pl.semaphore_signal(
+                barrier, inc=1, device_id={axis: lax.rem(me + d, n)}, device_id_type=MESH
+            )
+        count += n - 1
+    pl.semaphore_wait(barrier, count)
+
+
+def totals_kernel(n, x_ref, o_ref, recv, send_sem, recv_sem):
+    me = lax.axis_index("gene")
+    meet((("gene", n),))
+    copies = []
+    for d in range(1, n):
+        copies.append(
+            remote(
+                x_ref, recv.at[d - 1], send_sem.at[d - 1], recv_sem.at[d - 1],
+                {"gene": lax.rem(me + d, n)},
+            )
+        )
+        copies[-1].start()
+    total = x_ref[...]
+    for d in range(1, n):
+        copies[d - 1].wait()
+        total = total + recv[d - 1]
+    o_ref[...] = total
+
+
+def design_of(knot_ref, frac_ref, cov_ref):
+    slots = knot_ref.shape[1]
+    levels = lax.broadcasted_iota(jnp.int32, (SPL, slots), 0)
+    knot, frac = knot_ref[...], frac_ref[...]
+    hats = jnp.where(levels == knot, 1.0 - frac, 0.0)
+    hats = hats + jnp.where(levels == knot + 1, frac, 0.0)
+    return hats, cov_ref[...]
+
+
+def first_kernel(
+    counts_ref, totals_ref, batch_ref, live_ref, knot_ref, frac_ref, cov_ref, coef_ref, shift_ref,
+    factors_ref, loads_ref, g_ref, lin_ref, rhs, pair_hi, pair_lo, des_hi, des_lo, extra,
+):
+    slots = counts_ref.shape[1]
+
+    @pl.when(pl.program_id(0) == 0)
+    def _():
+        hats, cov = design_of(knot_ref, frac_ref, cov_ref)
+        ncov = cov.shape[0]
+        half = ncov // 2
+        design_hi, design_lo = split(jnp.concatenate([hats, cov], axis=0))
+        hot = lax.broadcasted_iota(jnp.int32, (BATCHES, slots), 0) == batch_ref[...]
+        hot = jnp.where(hot, 1.0, 0.0).astype(BF16)
+        width = SPL + ncov
+        rhs[0:width] = design_hi
+        rhs[width : 2 * width] = design_hi
+        rhs[2 * width : 3 * width] = design_lo
+        rhs[3 * width : 3 * width + BATCHES] = hot
+        rhs[3 * width + BATCHES : 3 * width + 2 * BATCHES] = hot
+
+        def put(at, block):
+            high, low = split(block)
+            pair_hi[at : at + block.shape[0]] = high
+            pair_lo[at : at + block.shape[0]] = low
+
+        at = 0
+        for p in range(SPL):
+            put(at, hats[p : p + 1] * cov)
+            at += ncov
+        for i in range(half):
+            put(at, cov[i : i + 1] * cov)
+            at += ncov
+        for i in range(half, ncov, 2):
+            put(
+                at,
+                jnp.concatenate(
+                    [cov[i : i + 1] * cov[half:], cov[i + 1 : i + 2] * cov[half:]], axis=0
+                ),
+            )
+            at += ncov
+        put(at, hats * hats)
+        at += SPL
+        later = jnp.concatenate([hats[1:], jnp.zeros((1, slots), F32)], axis=0)
+        put(at, hats * later)
+        at += SPL
+        put(at, jnp.zeros((width, slots), F32))
+        des_hi[...] = jnp.zeros(des_hi.shape, BF16)
+        des_lo[...] = jnp.zeros(des_lo.shape, BF16)
+        des_hi[128 - width : 128] = design_hi
+        des_lo[128 - width : 128] = design_lo
+        extra[0:1] = jnp.log((1.0 + totals_ref[...]) / GENES)
+        places = lax.broadcasted_iota(jnp.int32, (1, slots), 1)
+        extra[1:2] = jnp.where(places < live_ref[0], 1.0, 0.0)
+
+    coef_hi, coef_lo = split(coef_ref[...])
+    shift_hi, shift_lo = split(shift_ref[...])
+    lhs = jnp.concatenate([coef_hi, coef_lo, coef_hi, shift_hi, shift_lo], axis=1)
+    linear = mul(lhs, rhs[...], ACROSS) + mul(loads_ref[...], factors_ref[...], ROWS_BY_ROWS)
+    linear = linear + extra[0:1]
+    lin_ref[...] = linear
+    mask = extra[1:2]
+    expected = jnp.exp(linear)
+    w_hi, w_lo = split(expected * mask)
+    r_hi, r_lo = split((counts_ref[...].astype(F32) - expected) * mask)
+    gram = mul(w_hi, pair_hi[...], ROWS_BY_ROWS)
+    gram = gram + mul(w_hi, pair_lo[...], ROWS_BY_ROWS)
+    gram = gram + mul(w_lo, pair_hi[...], ROWS_BY_ROWS)
+    score = mul(r_hi, des_hi[...], ROWS_BY_ROWS)
+    score = score + mul(r_hi, des_lo[...], ROWS_BY_ROWS)
+    score = score + mul(r_lo, des_hi[...], ROWS_BY_ROWS)
+    blocks, rows, wide = g_ref.shape
+    g_ref[:, :, : wide - 128] = gram[:, : wide - 128].reshape(blocks, rows, wide - 128)
+    g_ref[:, :, wide - 128 :] = (gram[:, wide - 128 :] + score).reshape(blocks, rows, 128)
+
+
+def solve(g, x):
+    half = SPL // 2
+    cov_at, low_at, hat_at = SPL * SPL, SPL * SPL + half * SPL, SPL * SPL + half * SPL + half * half
+    off_at, score_at = hat_at + SPL, hat_at + 2 * SPL
+    spot = lax.broadcasted_iota(jnp.int32, (half, g.shape[1]), 0)
+
+    def one(block, i):
+        return block[i : i + 1]
+
+    lo = {}
+    hi = {}
+    for i in range(SPL):
+        unit = jnp.where(spot == i % half, ridge_weight, 0.0)
+        if i < half:
+            lo[i] = g[cov_at + i * SPL : cov_at + i * SPL + half] + unit
+            hi[i] = g[cov_at + i * SPL + half : cov_at + (i + 1) * SPL]
+        else:
+            hi[i] = g[low_at + (i - half) * half : low_at + (i - half + 1) * half] + unit
+    b_lo = g[score_at + SPL : score_at + SPL + half]
+    b_hi = g[score_at + SPL + half : score_at + 2 * SPL]
+    pivot_inv, edge, side_lo, side_hi, rest = [], [], [], [], []
+    for p in range(SPL):
+        d = g[hat_at + p : hat_at + p + 1] + ridge_weight
+        u_lo = g[p * SPL : p * SPL + half]
+        u_hi = g[p * SPL + half : (p + 1) * SPL]
+        b = g[score_at + p : score_at + p + 1]
+        if p > 0:
+            ratio = edge[-1] * pivot_inv[-1]
+            d = d - ratio * edge[-1]
+            u_lo = u_lo - ratio * side_lo[-1]
+            u_hi = u_hi - ratio * side_hi[-1]
+            b = b - ratio * rest[-1]
+        inv = 1.0 / d
+        pivot_inv.append(inv)
+        edge.append(g[off_at + p : off_at + p + 1])
+        side_lo.append(u_lo)
+        side_hi.append(u_hi)
+        rest.append(b)
+        scaled_lo, scaled_hi = u_lo * inv, u_hi * inv
+        b_lo = b_lo - scaled_lo * b
+        b_hi = b_hi - scaled_hi * b
+        for i in range(SPL):
+            if i < half:
+                f = one(scaled_lo, i)
+                lo[i] = lo[i] - f * u_lo
+            else:
+                f = one(scaled_hi, i - half)
+            hi[i] = hi[i] - f * u_hi
+    c_inv, c_rest = [], []
+    for j in range(SPL):
+        if j < half:
+            inv = 1.0 / one(lo[j], j)
+            b = one(b_lo, j)
+            s_lo = lo[j] * inv
+            b_lo = b_lo - s_lo * b
+        else:
+            inv = 1.0 / one(hi[j], j - half)
+            b = one(b_hi, j - half)
+        s_hi = hi[j] * inv
+        b_hi = b_hi - s_hi * b
+        c_inv.append(inv)
+        c_rest.append(b)
+        for i in range(j + 1, SPL):
+            if i < half:
+                f = one(s_lo, i)
+                lo[i] = lo[i] - f * lo[j]
+            else:
+                f = one(s_hi, i - half)
+            hi[i] = hi[i] - f * hi[j]
+    for j in reversed(range(SPL)):
+        found = c_rest[j] * c_inv[j]
+        x[SPL + j : SPL + j + 1] = found
+        for i in range(j):
+            c_rest[i] = c_rest[i] - (one(hi[i], j - half) if j >= half else one(lo[i], j)) * found
+    x_lo, x_hi = x[SPL : SPL + half], x[SPL + half : 2 * SPL]
+    after = None
+    for p in reversed(range(SPL)):
+        gone = jnp.sum(side_lo[p] * x_lo + side_hi[p] * x_hi, axis=0, keepdims=True)
+        b = rest[p] - gone
+        if after is not None:
+            b = b - edge[p] * after
+        after = b * pivot_inv[p]
+        x[p : p + 1] = after
+
+
+def newton_kernel(
+    n, g_ref, o_ref, from_pair, to_far, from_far, tall, turned, mine, theirs,
+    pair_send, pair_recv, far_send, far_recv, out_send, out_recv,
+):
+    me = lax.axis_index("cell")
+    core, chip = lax.rem(me, 2), me // 2
+    chips, rows, wide = n // 2, g_ref.shape[1], g_ref.shape[2]
+    meet((("cell", n),))
+    pair = []
+    for d in list(range(1, chips)) + [0]:
+        k = lax.rem(chip + d, chips)
+        pair.append(
+            remote(
+                g_ref.at[2 * k + 1 - core], from_pair.at[d], pair_send.at[d], pair_recv.at[d],
+                {"cell": me + 1 - 2 * core},
+            )
+        )
+        pair[-1].start()
+    far = []
+    for d in range(1, chips):
+        k = lax.rem(chip + d, chips)
+        pair[d - 1].wait()
+        to_far[d - 1] = g_ref[2 * k + core] + from_pair[d]
+        far.append(
+            remote(
+                to_far.at[d - 1], from_far.at[d - 1], far_send.at[d - 1], far_recv.at[d - 1],
+                {"cell": 2 * k + core},
+            )
+        )
+        far[-1].start()
+    pair[chips - 1].wait()
+    total = g_ref[me] + from_pair[0]
+    for d in range(1, chips):
+        far[d - 1].wait()
+        total = total + from_far[d - 1]
+    tall[0:rows] = total
+    if rows < 128:
+        tall[rows:128] = jnp.zeros((128 - rows, wide), F32)
+    turned[...] = tall[...].T
+    solve(turned, mine)
+    out = []
+    for d in range(1, n):
+        out.append(
+            remote(
+                mine, theirs.at[d - 1], out_send.at[d - 1], out_recv.at[d - 1],
+                {"cell": lax.rem(me + d, n)},
+            )
+        )
+        out[-1].start()
+    width = mine.shape[0]
+    fill = jnp.zeros((128 - width, 128), F32)
+
+    def put(owner, block):
+        o_ref[owner] = jnp.concatenate([block, fill], axis=0).T[:rows, :width]
+
+    put(me, mine[...])
+    for d in range(1, n):
+        out[d - 1].wait()
+        put(lax.rem(me + n - d, n), theirs[d - 1])
+
+
+def second_kernel(
+    counts_ref, lin_ref, live_ref, knot_ref, frac_ref, cov_ref, beta_ref, factors_ref, loads_ref,
+    gl_ref, gf_ref, rhs, mask_ref, f_one, f_hi, f_lo,
+):
+    slots = counts_ref.shape[1]
+    step = pl.program_id(0)
+
+    def spread(block):
+        wide = block.astype(F32)
+        zero = jnp.zeros(wide.shape, F32)
+        square_hi, square_lo = split(jnp.concatenate([zero, wide * wide], axis=1))
+        return jnp.concatenate([wide, zero], axis=1).astype(BF16), square_hi, square_lo
+
+    @pl.when(step == 0)
+    def _():
+        hats, cov = design_of(knot_ref, frac_ref, cov_ref)
+        design_hi, design_lo = split(jnp.concatenate([hats, cov], axis=0))
+        width = design_hi.shape[0]
+        rhs[0:width] = design_hi
+        rhs[width : 2 * width] = design_hi
+        rhs[2 * width : 3 * width] = design_lo
+        places = lax.broadcasted_iota(jnp.int32, (1, slots), 1)
+        mask_ref[0:1] = jnp.where(places < live_ref[0], 1.0, 0.0)
+        f_one[...], f_hi[...], f_lo[...] = spread(factors_ref[...])
+        gf_ref[...] = jnp.zeros(gf_ref.shape, F32)
+
+    blocks, rows, width = beta_ref.shape
+    beta_hi, beta_lo = split(beta_ref[...].reshape(blocks * rows, width))
+    delta = mul(jnp.concatenate([beta_hi, beta_lo, beta_hi], axis=1), rhs[...], ACROSS)
+    mask = mask_ref[0:1]
+    expected = jnp.exp(lin_ref[...] + delta)
+    w_hi, w_lo = split(expected * mask)
+    r_hi, r_lo = split((counts_ref[...].astype(F32) - expected) * mask)
+    gl = mul(r_hi, f_one[...], ACROSS) + mul(r_lo, f_one[...], ACROSS)
+    gl = gl + mul(w_hi, f_hi[...], ACROSS)
+    gl = gl + mul(w_hi, f_lo[...], ACROSS) + mul(w_lo, f_hi[...], ACROSS)
+    gl_ref[...] = gl.reshape(gl_ref.shape)
+    l_one, l_hi, l_lo = spread(loads_ref[...])
+    gf = mul(l_one, r_hi, DOWN) + mul(l_one, r_lo, DOWN)
+    gf = gf + mul(l_hi, w_hi, DOWN) + mul(l_lo, w_hi, DOWN) + mul(l_hi, w_lo, DOWN)
+    span = gf_ref.shape[2]
+    for j in range(gf_ref.shape[0]):
+        gf_ref[j] += gf[:, j * span : (j + 1) * span]
+
+
+def last_kernel(
+    n, m, gl_ref, gf_ref, ls_ref, fs_ref, from_c, my_l, their_l, from_g, my_f, their_f,
+    c_send, c_recv, g_send, g_recv, l_send, l_recv, f_send, f_recv,
+):
+    cell, gene = lax.axis_index("cell"), lax.axis_index("gene")
+    half = gl_ref.shape[2] // 2
+    span = gf_ref.shape[2]
+    meet((("cell", n), ("gene", m)))
+    across, along = [], []
+    for d in range(1, m):
+        to = lax.rem(gene + d, m)
+        along.append(
+            remote(gf_ref.at[to], from_g.at[d - 1], g_send.at[d - 1], g_recv.at[d - 1], {"gene": to})
+        )
+        along[-1].start()
+    for d in range(1, n):
+        to = lax.rem(cell + d, n)
+        across.append(
+            remote(gl_ref.at[to], from_c.at[d - 1], c_send.at[d - 1], c_recv.at[d - 1], {"cell": to})
+        )
+        across[-1].start()
+    total = gl_ref[cell]
+    for d in range(1, n):
+        across[d - 1].wait()
+        total = total + from_c[d - 1]
+    my_l[...] = total[:, :half] / jnp.sqrt(total[:, half:] + 1.0)
+    out_l, out_f = [], []
+    for d in range(1, n):
+        out_l.append(
+            remote(
+                my_l, their_l.at[d - 1], l_send.at[d - 1], l_recv.at[d - 1],
+                {"cell": lax.rem(cell + d, n)},
+            )
+        )
+        out_l[-1].start()
+    total = gf_ref[gene]
+    for d in range(1, m):
+        along[d - 1].wait()
+        total = total + from_g[d - 1]
+    my_f[...] = total[:half] / (total[half:] + 1.0)
+    for d in range(1, m):
+        out_f.append(
+            remote(
+                my_f, their_f.at[d - 1], f_send.at[d - 1], f_recv.at[d - 1],
+                {"gene": lax.rem(gene + d, m)},
+            )
+        )
+        out_f[-1].start()
+    ls_ref[cell] = my_l[...]
+    for d in range(1, n):
+        out_l[d - 1].wait()
+        ls_ref[lax.rem(cell + n - d, n)] = their_l[d - 1]
+    fill = jnp.zeros((half, span), F32)
+
+    def put(owner, block):
+        fs_ref[owner] = jnp.concatenate([block, fill], axis=0).T[:, :half]
+
+    put(gene, my_f[...])
+    for d in range(1, m):
+        out_f[d - 1].wait()
+        put(lax.rem(gene + m - d, m), their_f[d - 1])
+
+
+def local_fused(
+    n, m, counts, batch_id, live_cells, knot_bin, depth_frac, cell_covariates, coefficients,
+    batch_effect, factors, loadings,
+):
+    genes, slots = counts.shape
+    rows, span, latent = genes // n, slots // m, factors.shape[1]
+    ncov = cell_covariates.shape[0]
+    width = SPL + ncov
+    wide = SPL * ncov + ncov * ncov * 3 // 4 + 2 * SPL + width
+    steps = 2
+    tile, blocks = genes // steps, n // steps
+    dma = pltpu.SemaphoreType.DMA
+    shape = jax.ShapeDtypeStruct
+
+    def params(**kw):
+        return pltpu.CompilerParams(vmem_limit_bytes=LIMIT, **kw)
+
+    part = jnp.sum(counts, axis=0, keepdims=True).astype(F32)
+    totals = pl.pallas_call(
+        functools.partial(totals_kernel, m),
+        out_shape=shape((1, slots), F32),
+        in_specs=[VM],
+        out_specs=VM,
+        scratch_shapes=[pltpu.VMEM((m - 1, 1, slots), F32), dma((m - 1,)), dma((m - 1,))],
+        compiler_params=params(collective_id=0, has_side_effects=True),
+        name="totals",
+    )(part)
+
+    def by_rows(*tail):
+        return pl.BlockSpec((tile,) + tail, lambda i: (i,) + (0,) * len(tail))
+
+    def by_blocks(*tail):
+        return pl.BlockSpec((blocks,) + tail, lambda i: (i,) + (0,) * len(tail))
+
+    def whole(*dims):
+        return pl.BlockSpec(dims, lambda i: (0,) * len(dims))
+
+    smem = pl.BlockSpec(memory_space=pltpu.SMEM)
+    knot, frac, batch = (v.reshape(1, slots) for v in (knot_bin, depth_frac, batch_id))
+    line = whole(1, slots)
+    gram, lin = pl.pallas_call(
+        first_kernel,
+        grid=(steps,),
+        out_shape=(shape((n, rows, wide), F32), shape((genes, slots), F32)),
+        in_specs=[
+            by_rows(slots), line, line, smem, line, line, whole(ncov, slots),
+            by_rows(width), by_rows(BATCHES), whole(slots, latent), by_rows(latent),
+        ],
+        out_specs=(by_blocks(rows, wide), by_rows(slots)),
+        scratch_shapes=[
+            pltpu.VMEM((3 * width + 2 * BATCHES, slots), BF16),
+            pltpu.VMEM((wide, slots), BF16),
+            pltpu.VMEM((wide, slots), BF16),
+            pltpu.VMEM((128, slots), BF16),
+            pltpu.VMEM((128, slots), BF16),
+            pltpu.VMEM((8, slots), F32),
+        ],
+        compiler_params=params(),
+        name="first",
+    )(
+        counts, totals, batch, live_cells, knot, frac, cell_covariates, coefficients,
+        batch_effect, factors, loadings,
+    )
+    chips = n // 2
+    beta = pl.pallas_call(
+        functools.partial(newton_kernel, n),
+        out_shape=shape((n, rows, width), F32),
+        in_specs=[VM],
+        out_specs=VM,
+        scratch_shapes=[
+            pltpu.VMEM((chips, rows, wide), F32),
+            pltpu.VMEM((chips - 1, rows, wide), F32),
+            pltpu.VMEM((chips - 1, rows, wide), F32),
+            pltpu.VMEM((128, wide), F32),
+            pltpu.VMEM((wide, 128), F32),
+            pltpu.VMEM((width, 128), F32),
+            pltpu.VMEM((n - 1, width, 128), F32),
+            dma((chips,)), dma((chips,)), dma((chips - 1,)), dma((chips - 1,)),
+            dma((n - 1,)), dma((n - 1,)),
+        ],
+        compiler_params=params(collective_id=1, has_side_effects=True),
+        name="newton",
+    )(gram)
+    gl, gf = pl.pallas_call(
+        second_kernel,
+        grid=(steps,),
+        out_shape=(shape((n, rows, 2 * latent), F32), shape((m, 2 * latent, span), F32)),
+        in_specs=[
+            by_rows(slots), by_rows(slots), smem, line, line, whole(ncov, slots),
+            by_blocks(rows, width), whole(slots, latent), by_rows(latent),
+        ],
+        out_specs=(by_blocks(rows, 2 * latent), whole(m, 2 * latent, span)),
+        scratch_shapes=[
+            pltpu.VMEM((3 * width, slots), BF16),
+            pltpu.VMEM((8, slots), F32),
+            pltpu.VMEM((slots, 2 * latent), BF16),
+            pltpu.VMEM((slots, 2 * latent), BF16),
+            pltpu.VMEM((slots, 2 * latent), BF16),
+        ],
+        compiler_params=params(),
+        name="second",
+    )(counts, lin, live_cells, knot, frac, cell_covariates, beta, factors, loadings)
+    ls, fs = pl.pallas_call(
+        functools.partial(last_kernel, n, m),
+        out_shape=(shape((n, rows, latent), F32), shape((m, span, latent), F32)),
+        in_specs=[VM, VM],
+        out_specs=(VM, VM),
+        scratch_shapes=[
+            pltpu.VMEM((n - 1, rows, 2 * latent), F32),
+            pltpu.VMEM((rows, latent), F32),
+            pltpu.VMEM((n - 1, rows, latent), F32),
+            pltpu.VMEM((m - 1, 2 * latent, span), F32),
+            pltpu.VMEM((latent, span), F32),
+            pltpu.VMEM((m - 1, latent, span), F32),
+            dma((n - 1,)), dma((n - 1,)), dma((m - 1,)), dma((m - 1,)),
+            dma((n - 1,)), dma((n - 1,)), dma((m - 1,)), dma((m - 1,)),
+        ],
+        compiler_params=params(collective_id=2, has_side_effects=True),
+        name="last",
+    )(gl, gf)
+    return beta.reshape(genes, width), fs.reshape(slots, latent), ls.reshape(genes, latent)
+
+
+def local(n, m, *args):
+    counts, cov, factors = args[0], args[5], args[8]
+    genes, slots = counts.shape
+    fits = (
+        n % 2 == 0
+        and n > 2
+        and m > 1
+        and genes % (16 * n) == 0
+        and genes // n <= 128
+        and slots % (128 * m) == 0
+        and cov.shape[0] == SPL
+        and factors.shape[1] == 64
+    )
+    if fits:
+        return local_fused(n, m, *args)
+    return local_plain(*args)
+
+
 def solution(mesh):
     placed = (
         P("gene", "cell"),
@@ -101,7 +641,7 @@
         P("gene", None),
     )
     return jax.shard_map(
-        local,
+        functools.partial(local, mesh.shape["cell"], mesh.shape["gene"]),
         mesh=mesh,
         in_specs=placed,
         out_specs=(P("gene", None), P("cell", None), P("gene", None)),

time: 550 us -> 84.4 us (0.15)
  other arithmetic: 306 us -> 2.7 us
  waiting for transfers between devices: 159 us -> 0 us
  Pallas kernels: 0 us -> 71.9 us
  matrix products: 38.7 us -> 0 us
  blocking collectives: 22.7 us -> 0 us
  between operations: 14.7 us -> 1.41 us
    another operation x8 -> x0, other arithmetic: 295 us -> none  [the longest x4 282 us: newton_solve(): factor_lower = jnp.linalg.cholesky(system)]
    psum x2 -> x0, waiting for transfers between devices: 90.7 us -> none  [the longest x1 51.6 us: local(): grad_load, curv_load = lax.psum((grad_load, curv_load), 'cell')]
    pallas_call x0 -> x5, Pallas kernels: none -> 71.9 us  [the longest x1 24.3 us: local_fused(): pl.pallas_call(functools.partial(last_kernel, n, m), out_shape=(shape((n,...]
    reduce_scatter x1 -> x0, waiting for transfers between devices: 48.6 us -> none  [local(): lax.psum_scatter(gram_part, 'cell', scatter_dimension=0, tiled=True)]
    dot_general x8 -> x0, matrix products: 35 us -> none  [the longest x1 12 us: local(): gram_part = lax.dot_general(weight, pairs, contract, precision=highest)]
    unnamed x5 -> x0, waiting for transfers between devices: 19.3 us -> none
    psum x1 -> x0, blocking collectives: 13.5 us -> none  [local(): totals = lax.psum(jnp.sum(observed, axis=0), 'gene')]
    all_gather x1 -> x0, blocking collectives: 9.17 us -> none  [local(): beta_step = lax.all_gather(step_share, 'cell', axis=0, tiled=True)]
  transfers between devices with their start and end apart: 4 -> 0, of which waited for: 4 -> 0; matrix products, arithmetic and copies ran while one was open for 3% -> 0% of each run, Pallas kernels for 0% -> 0%
where the time goes in v1:
time: 84.4 us; the launch traced here: 84.1 us
  Pallas kernels  71.9 us (85%)
  local copies, waits for them, and re-layouts  8.06 us (10%)
  other arithmetic  2.7 us (3%)
  between operations  1.41 us (2%)
    pallas_call x1, Pallas kernels, local_fused(): pl.pallas_call(functools.partial(last_kernel, n, m), out_shape=(shape((n,...  24.3 us
    pallas_call x1, Pallas kernels, local_fused(): pl.pallas_call(functools.partial(newton_kernel, n), out_shape=shape((n, r...  21.4 us
    pallas_call x1, Pallas kernels, local_fused(): pl.pallas_call(first_kernel, grid=(steps,), out_shape=(shape((n, rows, wi...  9.13 us
    pallas_call x1, Pallas kernels, local_fused(): pl.pallas_call(functools.partial(totals_kernel, m), out_shape=shape((1, s...  8.6 us
    pallas_call x1, Pallas kernels, local_fused(): pl.pallas_call(second_kernel, grid=(steps,), out_shape=(shape((n, rows, 2...  8.46 us
    unnamed x17, local copies, waits for them, and re-layouts  8.06 us
    reduce_sum x1, other arithmetic, local_fused(): part = jnp.sum(counts, axis=0, keepdims=True).astype(F32)  2.11 us

profile of v1, /device:TPU:0, one launch (start us, length us, event | category | flops | bytes accessed | tf_op | source)
XLA Modules:
  0.0 84.1 jit_solution(14513146929376568057)
XLA Ops:
  0.6 0.0 copy-start.3
  0.6 0.0 copy-start.2
  0.7 0.0 copy-start.1
  0.7 0.0 copy-start.4
  1.4 2.1 %reduce_sum.9 = s32[1024]{0:T(1024)S(1)} reduce(s32[768,1024]{1,0:T(8,128)} %counts_ref.3, s32[]{:T(128)} %constant.0.clone.1), dimensions={0}, to_apply=%region_0.0 | reduce | flops 785408 | bytes 3149828 | tf_op jit(solution)/shard_map/reduce_sum | solution.py:506
  3.5 0.6 convert_element_type.5
  4.1 8.6 %totals.1.totals_ref = f32[1,1024]{1,0:T(1,128)} custom-call(f32[1,1024]{1,0:T(1,128)} %bitcast.14), custom_call_target="tpu_custom_call" | custom-call | tf_op jit(solution)/shard_map/totals/pallas_call | solution.py:507
  12.7 0.0 copy-done.3
  12.7 0.8 copy.16.loads_ref
  13.5 0.0 copy-done.2
  13.5 0.8 copy.15.factors_ref
  14.4 0.0 copy-done.4
  14.4 0.9 %copy.13.coef_ref = f32[768,32]{1,0:T(8,128)} copy(f32[768,32]{0,1:T(8,128)S(1)} %copy-done.4) | data formatting | bytes 196608 | tf_op args[6]
  15.3 0.0 copy-done.1
  15.3 0.9 %copy.14.shift_ref = f32[768,64]{1,0:T(8,128)} copy(f32[768,64]{0,1:T(8,128)S(1)} %copy-done.1) | data formatting | bytes 393216 | tf_op args[7]
  16.2 9.1 %first.1 = (f32[8,96,512]{2,1,0:T(8,128)}, f32[768,1024]{1,0:T(8,128)}) custom-call(s32[768,1024]{1,0:T(8,128)} %counts_ref.3, f32[1,1024]{1,0:T(1,128)} %totals.1.totals_ref, s32[1,1024]{1,0:T(1,128)} %bitcast.15, s32[1]{0:T(128)S(6)} %copy.22.live_ref, s32[1,1024]{1,0:T(1,128)} %bitcast.10, f32[1,1024]{1,0:T(1,128)} %bitcast.12, f32[16,1024]{1,0:T(8,128)} %cov_ref.3, ...), custom_call_target="tpu_custom_call" | custom-call | tf_op jit(solution)/shard_map/first/pallas_call | solution.py:529
  25.3 21.4 %newton.1.beta_ref = f32[8,96,32]{2,1,0:T(8,128)} custom-call(f32[8,96,512]{2,1,0:T(8,128)} %get-tuple-element.9.g_ref), custom_call_target="tpu_custom_call" | custom-call | tf_op jit(solution)/shard_map/newton/pallas_call | solution.py:553
  46.8 0.0 copy-start
  46.8 8.5 %second.1 = (f32[8,96,128]{2,1,0:T(8,128)}, f32[4,128,256]{2,1,0:T(8,128)}) custom-call(s32[768,1024]{1,0:T(8,128)} %counts_ref.3, f32[768,1024]{1,0:T(8,128)} %get-tuple-element.10.lin_ref, s32[1]{0:T(128)S(6)} %copy.22.live_ref, s32[1,1024]{1,0:T(1,128)} %bitcast.11, f32[1,1024]{1,0:T(1,128)} %bitcast.13, f32[16,1024]{1,0:T(8,128)} %cov_ref.3, ...), custom_call_target="tpu_custom_call" | custom-call | tf_op jit(solution)/shard_map/second/pallas_call | solution.py:572
  55.2 0.0 copy-done
  55.2 0.8 copy.19
  56.0 24.3 %last.1 = (f32[8,96,64]{2,1,0:T(8,128)}, f32[4,256,64]{2,1,0:T(8,128)}) custom-call(f32[8,96,128]{2,1,0:T(8,128)} %get-tuple-element.11.gl_ref, f32[4,128,256]{2,1,0:T(8,128)} %get-tuple-element.12.gf_ref), custom_call_target="tpu_custom_call" | custom-call | tf_op jit(solution)/shard_map/last/pallas_call | solution.py:591
  80.3 1.9 %copy.20 = f32[1024,64]{0,1:T(8,128)} copy(f32[1024,64]{1,0:T(8,128)} %bitcast.8) | data formatting | bytes 524288
  82.2 1.8 %copy.21 = f32[768,64]{0,1:T(8,128)} copy(f32[768,64]{1,0:T(8,128)} %bitcast.9) | data formatting | bytes 393216
Async XLA Ops:
  0.6 12.1 %copy-start.3 = (bf16[768,64]{0,1:T(8,128)(2,1)S(1)}, bf16[768,64]{0,1:T(8,128)(2,1)}, u32[]{:S(2)}) copy-start(bf16[768,64]{0,1:T(8,128)(2,1)} %param.19) | copy-start | bytes 294916
  0.6 12.9 %copy-start.2 = (bf16[1024,64]{0,1:T(8,128)(2,1)S(1)}, bf16[1024,64]{0,1:T(8,128)(2,1)}, u32[]{:S(2)}) copy-start(bf16[1024,64]{0,1:T(8,128)(2,1)} %param.18) | copy-start | bytes 393220
  0.7 14.6 %copy-start.1 = (f32[768,64]{0,1:T(8,128)S(1)}, f32[768,64]{0,1:T(8,128)}, u32[]{:S(2)}) copy-start(f32[768,64]{0,1:T(8,128)} %param.17) | copy-start | bytes 589828
  0.7 13.7 %copy-start.4 = (f32[768,32]{0,1:T(8,128)S(1)}, f32[768,32]{0,1:T(8,128)}, u32[]{:S(2)}) copy-start(f32[768,32]{0,1:T(8,128)} %param.16) | copy-start | bytes 294916
  46.8 8.5 %copy-start = (f32[8,96,32]{2,1,0:T(8,128)S(1)}, f32[8,96,32]{2,1,0:T(8,128)}, u32[]{:S(2)}) copy-start(f32[8,96,32]{2,1,0:T(8,128)} %newton.1.beta_ref) | copy-start | bytes 294916

commit v2 on v1

--- a/solution.py
+++ b/solution.py
@@ -176,6 +176,7 @@
         rhs[2 * width : 3 * width] = design_lo
         rhs[3 * width : 3 * width + BATCHES] = hot
         rhs[3 * width + BATCHES : 3 * width + 2 * BATCHES] = hot
+        rhs[3 * width + 2 * BATCHES :] = factors_ref[...]
 
         def put(at, block):
             high, low = split(block)
@@ -213,9 +214,8 @@
 
     coef_hi, coef_lo = split(coef_ref[...])
     shift_hi, shift_lo = split(shift_ref[...])
-    lhs = jnp.concatenate([coef_hi, coef_lo, coef_hi, shift_hi, shift_lo], axis=1)
-    linear = mul(lhs, rhs[...], ACROSS) + mul(loads_ref[...], factors_ref[...], ROWS_BY_ROWS)
-    linear = linear + extra[0:1]
+    lhs = jnp.concatenate([coef_hi, coef_lo, coef_hi, shift_hi, shift_lo, loads_ref[...]], axis=0)
+    linear = mul(lhs, rhs[...], DOWN) + extra[0:1]
     lin_ref[...] = linear
     mask = extra[1:2]
     expected = jnp.exp(linear)
@@ -380,7 +380,7 @@
 
 def second_kernel(
     counts_ref, lin_ref, live_ref, knot_ref, frac_ref, cov_ref, beta_ref, factors_ref, loads_ref,
-    gl_ref, gf_ref, rhs, mask_ref, f_one, f_hi, f_lo,
+    gl_ref, gf_ref, turned_ref, rhs, mask_ref, f_one, f_hi, f_lo,
 ):
     slots = counts_ref.shape[1]
     step = pl.program_id(0)
@@ -388,8 +388,8 @@
     def spread(block):
         wide = block.astype(F32)
         zero = jnp.zeros(wide.shape, F32)
-        square_hi, square_lo = split(jnp.concatenate([zero, wide * wide], axis=1))
-        return jnp.concatenate([wide, zero], axis=1).astype(BF16), square_hi, square_lo
+        square_hi, square_lo = split(jnp.concatenate([zero, wide * wide], axis=0))
+        return jnp.concatenate([wide, zero], axis=0).astype(BF16), square_hi, square_lo
 
     @pl.when(step == 0)
     def _():
@@ -405,19 +405,22 @@
         gf_ref[...] = jnp.zeros(gf_ref.shape, F32)
 
     blocks, rows, width = beta_ref.shape
-    beta_hi, beta_lo = split(beta_ref[...].reshape(blocks * rows, width))
+    beta = beta_ref[...].reshape(blocks * rows, width)
+    beta_hi, beta_lo = split(beta)
+    fill = jnp.zeros((blocks * rows, 128 - width), F32)
+    turned_ref[...] = jnp.concatenate([beta, fill], axis=1).T[:width]
     delta = mul(jnp.concatenate([beta_hi, beta_lo, beta_hi], axis=1), rhs[...], ACROSS)
     mask = mask_ref[0:1]
     expected = jnp.exp(lin_ref[...] + delta)
     w_hi, w_lo = split(expected * mask)
     r_hi, r_lo = split((counts_ref[...].astype(F32) - expected) * mask)
-    gl = mul(r_hi, f_one[...], ACROSS) + mul(r_lo, f_one[...], ACROSS)
-    gl = gl + mul(w_hi, f_hi[...], ACROSS)
-    gl = gl + mul(w_hi, f_lo[...], ACROSS) + mul(w_lo, f_hi[...], ACROSS)
+    gl = mul(r_hi, f_one[...], ROWS_BY_ROWS) + mul(r_lo, f_one[...], ROWS_BY_ROWS)
+    gl = gl + mul(w_hi, f_hi[...], ROWS_BY_ROWS)
+    gl = gl + mul(w_hi, f_lo[...], ROWS_BY_ROWS) + mul(w_lo, f_hi[...], ROWS_BY_ROWS)
     gl_ref[...] = gl.reshape(gl_ref.shape)
     l_one, l_hi, l_lo = spread(loads_ref[...])
-    gf = mul(l_one, r_hi, DOWN) + mul(l_one, r_lo, DOWN)
-    gf = gf + mul(l_hi, w_hi, DOWN) + mul(l_lo, w_hi, DOWN) + mul(l_hi, w_lo, DOWN)
+    gf = mul(l_one, r_hi, ACROSS) + mul(l_one, r_lo, ACROSS)
+    gf = gf + mul(l_hi, w_hi, ACROSS) + mul(l_lo, w_hi, ACROSS) + mul(l_hi, w_lo, ACROSS)
     span = gf_ref.shape[2]
     for j in range(gf_ref.shape[0]):
         gf_ref[j] += gf[:, j * span : (j + 1) * span]
@@ -449,11 +452,12 @@
         across[d - 1].wait()
         total = total + from_c[d - 1]
     my_l[...] = total[:, :half] / jnp.sqrt(total[:, half:] + 1.0)
+    their_l[cell] = my_l[...]
     out_l, out_f = [], []
     for d in range(1, n):
         out_l.append(
             remote(
-                my_l, their_l.at[d - 1], l_send.at[d - 1], l_recv.at[d - 1],
+                my_l, their_l.at[cell], l_send.at[d - 1], l_recv.at[d - 1],
                 {"cell": lax.rem(cell + d, n)},
             )
         )
@@ -471,16 +475,14 @@
             )
         )
         out_f[-1].start()
-    ls_ref[cell] = my_l[...]
+    def put(owner, block):
+        fs_ref[:, pl.ds(pl.multiple_of(owner * span, span), span)] = block
+
+    put(gene, my_f[...])
     for d in range(1, n):
         out_l[d - 1].wait()
-        ls_ref[lax.rem(cell + n - d, n)] = their_l[d - 1]
-    fill = jnp.zeros((half, span), F32)
-
-    def put(owner, block):
-        fs_ref[owner] = jnp.concatenate([block, fill], axis=0).T[:, :half]
-
-    put(gene, my_f[...])
+    found = their_l[...].reshape(ls_ref.shape[1], half)
+    ls_ref[...] = jnp.concatenate([found, jnp.zeros(found.shape, F32)], axis=1).T[:half]
     for d in range(1, m):
         out_f[d - 1].wait()
         put(lax.rem(gene + m - d, m), their_f[d - 1])
@@ -517,6 +519,9 @@
     def by_rows(*tail):
         return pl.BlockSpec((tile,) + tail, lambda i: (i,) + (0,) * len(tail))
 
+    def by_lanes(count):
+        return pl.BlockSpec((count, tile), lambda i: (0, i))
+
     def by_blocks(*tail):
         return pl.BlockSpec((blocks,) + tail, lambda i: (i,) + (0,) * len(tail))
 
@@ -532,11 +537,11 @@
         out_shape=(shape((n, rows, wide), F32), shape((genes, slots), F32)),
         in_specs=[
             by_rows(slots), line, line, smem, line, line, whole(ncov, slots),
-            by_rows(width), by_rows(BATCHES), whole(slots, latent), by_rows(latent),
+            by_lanes(width), by_lanes(BATCHES), whole(latent, slots), by_lanes(latent),
         ],
         out_specs=(by_blocks(rows, wide), by_rows(slots)),
         scratch_shapes=[
-            pltpu.VMEM((3 * width + 2 * BATCHES, slots), BF16),
+            pltpu.VMEM((3 * width + 2 * BATCHES + latent, slots), BF16),
             pltpu.VMEM((wide, slots), BF16),
             pltpu.VMEM((wide, slots), BF16),
             pltpu.VMEM((128, slots), BF16),
@@ -546,8 +551,8 @@
         compiler_params=params(),
         name="first",
     )(
-        counts, totals, batch, live_cells, knot, frac, cell_covariates, coefficients,
-        batch_effect, factors, loadings,
+        counts, totals, batch, live_cells, knot, frac, cell_covariates, coefficients.T,
+        batch_effect.T, factors.T, loadings.T,
     )
     chips = n // 2
     beta = pl.pallas_call(
@@ -569,34 +574,35 @@
         compiler_params=params(collective_id=1, has_side_effects=True),
         name="newton",
     )(gram)
-    gl, gf = pl.pallas_call(
+    gl, gf, beta_turned = pl.pallas_call(
         second_kernel,
         grid=(steps,),
-        out_shape=(shape((n, rows, 2 * latent), F32), shape((m, 2 * latent, span), F32)),
+        out_shape=(shape((n, rows, 2 * latent), F32), shape((m, 2 * latent, span), F32),
+                   shape((width, genes), F32)),
         in_specs=[
             by_rows(slots), by_rows(slots), smem, line, line, whole(ncov, slots),
-            by_blocks(rows, width), whole(slots, latent), by_rows(latent),
+            by_blocks(rows, width), whole(latent, slots), by_lanes(latent),
         ],
-        out_specs=(by_blocks(rows, 2 * latent), whole(m, 2 * latent, span)),
+        out_specs=(by_blocks(rows, 2 * latent), whole(m, 2 * latent, span), by_lanes(width)),
         scratch_shapes=[
             pltpu.VMEM((3 * width, slots), BF16),
             pltpu.VMEM((8, slots), F32),
-            pltpu.VMEM((slots, 2 * latent), BF16),
-            pltpu.VMEM((slots, 2 * latent), BF16),
-            pltpu.VMEM((slots, 2 * latent), BF16),
+            pltpu.VMEM((2 * latent, slots), BF16),
+            pltpu.VMEM((2 * latent, slots), BF16),
+            pltpu.VMEM((2 * latent, slots), BF16),
         ],
         compiler_params=params(),
         name="second",
-    )(counts, lin, live_cells, knot, frac, cell_covariates, beta, factors, loadings)
+    )(counts, lin, live_cells, knot, frac, cell_covariates, beta, factors.T, loadings.T)
     ls, fs = pl.pallas_call(
         functools.partial(last_kernel, n, m),
-        out_shape=(shape((n, rows, latent), F32), shape((m, span, latent), F32)),
+        out_shape=(shape((latent, genes), F32), shape((latent, slots), F32)),
         in_specs=[VM, VM],
         out_specs=(VM, VM),
         scratch_shapes=[
             pltpu.VMEM((n - 1, rows, 2 * latent), F32),
             pltpu.VMEM((rows, latent), F32),
-            pltpu.VMEM((n - 1, rows, latent), F32),
+            pltpu.VMEM((n, rows, latent), F32),
             pltpu.VMEM((m - 1, 2 * latent, span), F32),
             pltpu.VMEM((latent, span), F32),
             pltpu.VMEM((m - 1, latent, span), F32),
@@ -606,7 +612,7 @@
         compiler_params=params(collective_id=2, has_side_effects=True),
         name="last",
     )(gl, gf)
-    return beta.reshape(genes, width), fs.reshape(slots, latent), ls.reshape(genes, latent)
+    return beta_turned.T, fs.T, ls.T
 
 
 def local(n, m, *args):

time: 84.4 us -> 78.6 us (0.931)
  local copies, waits for them, and re-layouts: 8.06 us -> 3.29 us
  Pallas kernels: 71.9 us -> 71 us
    unnamed x17 -> x2, local copies, waits for them, and re-layouts: 8.06 us -> 3.29 us
where the time goes in v2:
time: 78.6 us; the launch traced here: 78.3 us
  Pallas kernels  71 us (90%)
  local copies, waits for them, and re-layouts  3.29 us (4%)
  other arithmetic  2.7 us (3%)
  between operations  1.3 us (2%)
    pallas_call x1, Pallas kernels, local_fused(): pl.pallas_call(functools.partial(last_kernel, n, m), out_shape=(shape((la...  23.9 us
    pallas_call x1, Pallas kernels, local_fused(): pl.pallas_call(functools.partial(newton_kernel, n), out_shape=shape((n, r...  21.4 us
    pallas_call x1, Pallas kernels, local_fused(): pl.pallas_call(first_kernel, grid=(steps,), out_shape=(shape((n, rows, wi...  8.87 us
    pallas_call x1, Pallas kernels, local_fused(): pl.pallas_call(functools.partial(totals_kernel, m), out_shape=shape((1, s...  8.6 us
    pallas_call x1, Pallas kernels, local_fused(): pl.pallas_call(second_kernel, grid=(steps,), out_shape=(shape((n, rows, 2...  8.17 us
    unnamed x2, local copies, waits for them, and re-layouts  3.29 us
    reduce_sum x1, other arithmetic, local_fused(): part = jnp.sum(counts, axis=0, keepdims=True).astype(F32)  2.11 us

profile of v2, /device:TPU:0, one launch (start us, length us, event | category | flops | bytes accessed | tf_op | source)
XLA Modules:
  0.0 78.3 jit_solution(9221637131199953624)
XLA Ops:
  1.3 2.1 %reduce_sum.9 = s32[1024]{0:T(1024)S(1)} reduce(s32[768,1024]{1,0:T(8,128)} %counts_ref.3, s32[]{:T(128)} %constant.0.clone.1), dimensions={0}, to_apply=%region_0.0 | reduce | flops 785408 | bytes 3149828 | tf_op jit(solution)/shard_map/reduce_sum | solution.py:508
  3.4 0.6 convert_element_type.5
  4.0 8.6 %totals.1.totals_ref = f32[1,1024]{1,0:T(1,128)} custom-call(f32[1,1024]{1,0:T(1,128)} %bitcast.19), custom_call_target="tpu_custom_call" | custom-call | tf_op jit(solution)/shard_map/totals/pallas_call | solution.py:509
  12.6 8.9 %first.1 = (f32[8,96,512]{2,1,0:T(8,128)}, f32[768,1024]{1,0:T(8,128)}) custom-call(s32[768,1024]{1,0:T(8,128)} %counts_ref.3, f32[1,1024]{1,0:T(1,128)} %totals.1.totals_ref, s32[1,1024]{1,0:T(1,128)} %bitcast.24, s32[1]{0:T(128)S(6)} %copy.15.live_ref, s32[1,1024]{1,0:T(1,128)} %bitcast.20, f32[1,1024]{1,0:T(1,128)} %bitcast.22, f32[16,1024]{1,0:T(8,128)} %cov_ref.3, ...), custom_call_target="tpu_custom_call" | custom-call | tf_op jit(solution)/shard_map/first/pallas_call | solution.py:534
  21.5 21.4 %newton.1.beta_ref = f32[8,96,32]{2,1,0:T(8,128)} custom-call(f32[8,96,512]{2,1,0:T(8,128)} %get-tuple-element.11.g_ref), custom_call_target="tpu_custom_call" | custom-call | tf_op jit(solution)/shard_map/newton/pallas_call | solution.py:558
  42.9 8.2 %second.1 = (f32[8,96,128]{2,1,0:T(8,128)}, f32[4,128,256]{2,1,0:T(8,128)}, f32[32,768]{1,0:T(8,128)}) custom-call(s32[768,1024]{1,0:T(8,128)} %counts_ref.3, f32[768,1024]{1,0:T(8,128)} %get-tuple-element.10.lin_ref, s32[1]{0:T(128)S(6)} %copy.15.live_ref, s32[1,1024]{1,0:T(1,128)} %bitcast.21, f32[1,1024]{1,0:T(1,128)} %bitcast.23, f32[16,1024]{1,0:T(8,128)} %cov_ref.3, ...), custom_call_target="tpu_custom_call" | custom-call | tf_op jit(solution)/shard_map/second/pallas_call | solution.py:577
  51.0 23.9 %last.1 = (f32[64,768]{1,0:T(8,128)}, f32[64,1024]{1,0:T(8,128)}) custom-call(f32[8,96,128]{2,1,0:T(8,128)} %get-tuple-element.13.gl_ref, f32[4,128,256]{2,1,0:T(8,128)} %get-tuple-element.14.gf_ref), custom_call_target="tpu_custom_call" | custom-call | tf_op jit(solution)/shard_map/last/pallas_call | solution.py:597
  75.0 1.7 %copy.16 = f32[1024,64]{0,1:T(8,128)} copy(f32[1024,64]{0,1:T(8,128)} %bitcast.15) | data formatting | bytes 524288
  76.7 1.6 %copy.17 = f32[768,64]{0,1:T(8,128)} copy(f32[768,64]{0,1:T(8,128)} %bitcast.17) | data formatting | bytes 393216

commit v3 on v2

--- a/solution.py
+++ b/solution.py
@@ -378,69 +378,66 @@
         put(lax.rem(me + n - d, n), theirs[d - 1])
 
 
-def second_kernel(
-    counts_ref, lin_ref, live_ref, knot_ref, frac_ref, cov_ref, beta_ref, factors_ref, loads_ref,
-    gl_ref, gf_ref, turned_ref, rhs, mask_ref, f_one, f_hi, f_lo,
-):
-    slots = counts_ref.shape[1]
-    step = pl.program_id(0)
-
-    def spread(block):
-        wide = block.astype(F32)
-        zero = jnp.zeros(wide.shape, F32)
-        square_hi, square_lo = split(jnp.concatenate([zero, wide * wide], axis=0))
-        return jnp.concatenate([wide, zero], axis=0).astype(BF16), square_hi, square_lo
-
-    @pl.when(step == 0)
-    def _():
-        hats, cov = design_of(knot_ref, frac_ref, cov_ref)
-        design_hi, design_lo = split(jnp.concatenate([hats, cov], axis=0))
-        width = design_hi.shape[0]
-        rhs[0:width] = design_hi
-        rhs[width : 2 * width] = design_hi
-        rhs[2 * width : 3 * width] = design_lo
-        places = lax.broadcasted_iota(jnp.int32, (1, slots), 1)
-        mask_ref[0:1] = jnp.where(places < live_ref[0], 1.0, 0.0)
-        f_one[...], f_hi[...], f_lo[...] = spread(factors_ref[...])
-        gf_ref[...] = jnp.zeros(gf_ref.shape, F32)
-
-    blocks, rows, width = beta_ref.shape
-    beta = beta_ref[...].reshape(blocks * rows, width)
-    beta_hi, beta_lo = split(beta)
-    fill = jnp.zeros((blocks * rows, 128 - width), F32)
-    turned_ref[...] = jnp.concatenate([beta, fill], axis=1).T[:width]
-    delta = mul(jnp.concatenate([beta_hi, beta_lo, beta_hi], axis=1), rhs[...], ACROSS)
-    mask = mask_ref[0:1]
-    expected = jnp.exp(lin_ref[...] + delta)
-    w_hi, w_lo = split(expected * mask)
-    r_hi, r_lo = split((counts_ref[...].astype(F32) - expected) * mask)
-    gl = mul(r_hi, f_one[...], ROWS_BY_ROWS) + mul(r_lo, f_one[...], ROWS_BY_ROWS)
-    gl = gl + mul(w_hi, f_hi[...], ROWS_BY_ROWS)
-    gl = gl + mul(w_hi, f_lo[...], ROWS_BY_ROWS) + mul(w_lo, f_hi[...], ROWS_BY_ROWS)
-    gl_ref[...] = gl.reshape(gl_ref.shape)
-    l_one, l_hi, l_lo = spread(loads_ref[...])
-    gf = mul(l_one, r_hi, ACROSS) + mul(l_one, r_lo, ACROSS)
-    gf = gf + mul(l_hi, w_hi, ACROSS) + mul(l_lo, w_hi, ACROSS) + mul(l_hi, w_lo, ACROSS)
-    span = gf_ref.shape[2]
-    for j in range(gf_ref.shape[0]):
-        gf_ref[j] += gf[:, j * span : (j + 1) * span]
+def spread(block):
+    wide = block.astype(F32)
+    zero = jnp.zeros(wide.shape, F32)
+    square_hi, square_lo = split(jnp.concatenate([zero, wide * wide], axis=0))
+    return jnp.concatenate([wide, zero], axis=0).astype(BF16), square_hi, square_lo
 
 
 def last_kernel(
-    n, m, gl_ref, gf_ref, ls_ref, fs_ref, from_c, my_l, their_l, from_g, my_f, their_f,
+    n, m, counts_ref, lin_ref, live_ref, knot_ref, frac_ref, cov_ref, beta_ref, factors_ref,
+    loads_ref, ls_ref, fs_ref, rhs, mask_ref, f_one, f_hi, f_lo, gl_ref, gf_ref,
+    from_c, my_l, their_l, from_g, my_f, their_f,
     c_send, c_recv, g_send, g_recv, l_send, l_recv, f_send, f_recv,
 ):
     cell, gene = lax.axis_index("cell"), lax.axis_index("gene")
     half = gl_ref.shape[2] // 2
     span = gf_ref.shape[2]
+    slots = counts_ref.shape[1]
+    hats, cov = design_of(knot_ref, frac_ref, cov_ref)
+    design_hi, design_lo = split(jnp.concatenate([hats, cov], axis=0))
+    width = design_hi.shape[0]
+    rhs[0:width] = design_hi
+    rhs[width : 2 * width] = design_hi
+    rhs[2 * width : 3 * width] = design_lo
+    places = lax.broadcasted_iota(jnp.int32, (1, slots), 1)
+    mask_ref[0:1] = jnp.where(places < live_ref[...], 1.0, 0.0)
+    f_one[...], f_hi[...], f_lo[...] = spread(factors_ref[...])
+    blocks, rows, _ = beta_ref.shape
+    beta_hi, beta_lo = split(beta_ref[...].reshape(blocks * rows, width))
+    lhs = jnp.concatenate([beta_hi, beta_lo, beta_hi], axis=1)
+    l_one, l_hi, l_lo = spread(loads_ref[...])
     meet((("cell", n), ("gene", m)))
     across, along = [], []
-    for d in range(1, m):
+    for d in list(range(1, m)) + [0]:
         to = lax.rem(gene + d, m)
-        along.append(
-            remote(gf_ref.at[to], from_g.at[d - 1], g_send.at[d - 1], g_recv.at[d - 1], {"gene": to})
-        )
-        along[-1].start()
+        cols = pl.ds(pl.multiple_of(to * span, span), span)
+        delta = mul(lhs, rhs[:, cols], ACROSS)
+        mask = mask_ref[0:1, cols]
+        expected = jnp.exp(lin_ref[:, cols] + delta)
+        w_hi, w_lo = split(expected * mask)
+        r_hi, r_lo = split((counts_ref[:, cols].astype(F32) - expected) * mask)
+        gf = mul(l_one, r_hi, ACROSS) + mul(l_one, r_lo, ACROSS)
+        gf = gf + mul(l_hi, w_hi, ACROSS) + mul(l_lo, w_hi, ACROSS) + mul(l_hi, w_lo, ACROSS)
+        gf_ref[d] = gf
+        if d > 0:
+            along.append(
+                remote(
+                    gf_ref.at[d], from_g.at[d - 1], g_send.at[d - 1], g_recv.at[d - 1],
+                    {"gene": to},
+                )
+            )
+            along[-1].start()
+        one, high, low = f_one[:, cols], f_hi[:, cols], f_lo[:, cols]
+        gl = mul(r_hi, one, ROWS_BY_ROWS) + mul(r_lo, one, ROWS_BY_ROWS)
+        gl = gl + mul(w_hi, high, ROWS_BY_ROWS)
+        gl = gl + mul(w_hi, low, ROWS_BY_ROWS) + mul(w_lo, high, ROWS_BY_ROWS)
+        gl = gl.reshape(gl_ref.shape)
+        if d == 1:
+            gl_ref[...] = gl
+        else:
+            gl_ref[...] += gl
     for d in range(1, n):
         to = lax.rem(cell + d, n)
         across.append(
@@ -462,7 +459,7 @@
             )
         )
         out_l[-1].start()
-    total = gf_ref[gene]
+    total = gf_ref[0]
     for d in range(1, m):
         along[d - 1].wait()
         total = total + from_g[d - 1]
@@ -574,32 +571,19 @@
         compiler_params=params(collective_id=1, has_side_effects=True),
         name="newton",
     )(gram)
-    gl, gf, beta_turned = pl.pallas_call(
-        second_kernel,
-        grid=(steps,),
-        out_shape=(shape((n, rows, 2 * latent), F32), shape((m, 2 * latent, span), F32),
-                   shape((width, genes), F32)),
-        in_specs=[
-            by_rows(slots), by_rows(slots), smem, line, line, whole(ncov, slots),
-            by_blocks(rows, width), whole(latent, slots), by_lanes(latent),
-        ],
-        out_specs=(by_blocks(rows, 2 * latent), whole(m, 2 * latent, span), by_lanes(width)),
+    ls, fs = pl.pallas_call(
+        functools.partial(last_kernel, n, m),
+        out_shape=(shape((latent, genes), F32), shape((latent, slots), F32)),
+        in_specs=[VM] * 9,
+        out_specs=(VM, VM),
         scratch_shapes=[
             pltpu.VMEM((3 * width, slots), BF16),
             pltpu.VMEM((8, slots), F32),
             pltpu.VMEM((2 * latent, slots), BF16),
             pltpu.VMEM((2 * latent, slots), BF16),
             pltpu.VMEM((2 * latent, slots), BF16),
-        ],
-        compiler_params=params(),
-        name="second",
-    )(counts, lin, live_cells, knot, frac, cell_covariates, beta, factors.T, loadings.T)
-    ls, fs = pl.pallas_call(
-        functools.partial(last_kernel, n, m),
-        out_shape=(shape((latent, genes), F32), shape((latent, slots), F32)),
-        in_specs=[VM, VM],
-        out_specs=(VM, VM),
-        scratch_shapes=[
+            pltpu.VMEM((n, rows, 2 * latent), F32),
+            pltpu.VMEM((m, 2 * latent, span), F32),
             pltpu.VMEM((n - 1, rows, 2 * latent), F32),
             pltpu.VMEM((rows, latent), F32),
             pltpu.VMEM((n, rows, latent), F32),
@@ -611,8 +595,11 @@
         ],
         compiler_params=params(collective_id=2, has_side_effects=True),
         name="last",
-    )(gl, gf)
-    return beta_turned.T, fs.T, ls.T
+    )(
+        counts, lin, live_cells.reshape(1, 1), knot, frac, cell_covariates, beta,
+        factors.T, loadings.T,
+    )
+    return beta.reshape(genes, width), fs.T, ls.T
 
 
 def local(n, m, *args):

time: 78.6 us -> 73.8 us (0.939)
  Pallas kernels: 71 us -> 65.4 us
    pallas_call x1 -> x0, Pallas kernels: 8.17 us -> none  [local_fused(): pl.pallas_call(second_kernel, grid=(steps,), out_shape=(shape((n, rows, 2...]
    pallas_call x1, Pallas kernels: 23.9 us -> 26.5 us  [local_fused(): pl.pallas_call(functools.partial(last_kernel, n, m), out_shape=(shape((la...]
    unnamed x2 -> x5, local copies, waits for them, and re-layouts: 3.29 us -> 4.07 us
where the time goes in v3:
time: 73.8 us; the launch traced here: 73.5 us
  Pallas kernels  65.4 us (89%)
  local copies, waits for them, and re-layouts  4.07 us (6%)
  other arithmetic  2.7 us (4%)
  between operations  1.32 us (2%)
    pallas_call x1, Pallas kernels, local_fused(): pl.pallas_call(functools.partial(last_kernel, n, m), out_shape=(shape((la...  26.5 us
    pallas_call x1, Pallas kernels, local_fused(): pl.pallas_call(functools.partial(newton_kernel, n), out_shape=shape((n, r...  21.4 us
    pallas_call x1, Pallas kernels, local_fused(): pl.pallas_call(first_kernel, grid=(steps,), out_shape=(shape((n, rows, wi...  8.87 us
    pallas_call x1, Pallas kernels, local_fused(): pl.pallas_call(functools.partial(totals_kernel, m), out_shape=shape((1, s...  8.6 us
    unnamed x5, local copies, waits for them, and re-layouts  4.07 us
    reduce_sum x1, other arithmetic, local_fused(): part = jnp.sum(counts, axis=0, keepdims=True).astype(F32)  2.11 us

profile of v3, /device:TPU:0, one launch (start us, length us, event | category | flops | bytes accessed | tf_op | source)
XLA Modules:
  0.0 73.5 jit_solution(3249578162455704482)
XLA Ops:
  1.3 2.1 %reduce_sum.9 = s32[1024]{0:T(1024)S(1)} reduce(s32[768,1024]{1,0:T(8,128)} %counts_ref.3, s32[]{:T(128)} %constant.0.clone.1), dimensions={0}, to_apply=%region_0.0 | reduce | flops 785408 | bytes 3149828 | tf_op jit(solution)/shard_map/reduce_sum | solution.py:505
  3.4 0.6 convert_element_type.5
  4.0 8.6 %totals.1.totals_ref = f32[1,1024]{1,0:T(1,128)} custom-call(f32[1,1024]{1,0:T(1,128)} %bitcast.22), custom_call_target="tpu_custom_call" | custom-call | tf_op jit(solution)/shard_map/totals/pallas_call | solution.py:506
  12.6 8.9 %first.1 = (f32[8,96,512]{2,1,0:T(8,128)}, f32[768,1024]{1,0:T(8,128)}) custom-call(s32[768,1024]{1,0:T(8,128)} %counts_ref.3, f32[1,1024]{1,0:T(1,128)} %totals.1.totals_ref, s32[1,1024]{1,0:T(1,128)} %bitcast.27, s32[1]{0:T(128)} %copy.16.live_ref, s32[1,1024]{1,0:T(1,128)} %bitcast.23, f32[1,1024]{1,0:T(1,128)} %bitcast.25, f32[16,1024]{1,0:T(8,128)} %cov_ref.3, ...), custom_call_target="tpu_custom_call" | custom-call | tf_op jit(solution)/shard_map/first/pallas_call | solution.py:531
  21.5 21.4 %newton.1.beta_ref = f32[8,96,32]{2,1,0:T(8,128)} custom-call(f32[8,96,512]{2,1,0:T(8,128)} %get-tuple-element.7.g_ref), custom_call_target="tpu_custom_call" | custom-call | tf_op jit(solution)/shard_map/newton/pallas_call | solution.py:555
  42.9 0.0 copy-start
  42.9 26.5 %last.1 = (f32[64,768]{1,0:T(8,128)}, f32[64,1024]{1,0:T(8,128)}) custom-call(s32[768,1024]{1,0:T(8,128)} %counts_ref.3, f32[768,1024]{1,0:T(8,128)} %get-tuple-element.8.lin_ref, s32[1,1]{1,0:T(1,128)} %bitcast.12.live_ref, s32[1,1024]{1,0:T(1,128)} %bitcast.24, f32[1,1024]{1,0:T(1,128)} %bitcast.26, f32[16,1024]{1,0:T(8,128)} %cov_ref.3, ...), custom_call_target="tpu_custom_call" | custom-call | tf_op jit(solution)/shard_map/last/pallas_call | solution.py:574
  69.4 0.0 copy-done
  69.4 0.8 %copy.13 = f32[768,32]{0,1:T(8,128)} copy(f32[768,32]{1,0:T(8,128)S(1)} %bitcast.13) | data formatting | bytes 196608
  70.2 1.7 %copy.17 = f32[1024,64]{0,1:T(8,128)} copy(f32[1024,64]{0,1:T(8,128)} %bitcast.18) | data formatting | bytes 524288
  71.9 1.6 %copy.18 = f32[768,64]{0,1:T(8,128)} copy(f32[768,64]{0,1:T(8,128)} %bitcast.20) | data formatting | bytes 393216
Async XLA Ops:
  42.9 26.5 %copy-start = (f32[8,96,32]{2,1,0:T(8,128)S(1)}, f32[8,96,32]{2,1,0:T(8,128)}, u32[]{:S(2)}) copy-start(f32[8,96,32]{2,1,0:T(8,128)} %newton.1.beta_ref) | copy-start | bytes 294916
